TPU v7x, 32 devices: a whole 2x2x4 slice. The times are simulated.
32 devices in a mesh: dp: 8 (over z, core), ctx: 4 (over y, x).
Axes of the slice: x: 2, y: 2, z: 4, core: 2. Of those that a mesh axis runs over, the one named last changes fastest.
Arguments:
- qkv: bfloat16 [8, 512, 5120], P('dp', 'ctx'), may hold values from -8 to 8
- dest: int32 [8, 8], P('dp'), may hold values from 0 to 7, as said below
- order: int32 [8], replicated, may hold values from 0 to 7, as said below
- lengths: int32 [8, 8], replicated, may hold values from 1 to 256, 512 in all within a row
Outputs:
- attended: bfloat16 [8, 512, 4096], P('dp', 'ctx')
Inputs may be any that keep to these rules, and one draw needn't show every extreme that they name: `dest`: entry [r, s] is r itself, r + 1 or r - 1 (indices modulo 8), and the relation is mutual: if entry [r, s] is t, entry [t, s] is r. For every c below 4: order[2 c] is below 4 and order[2 c + 1] = 7 - order[2 c]; every span appears once.
All inputs are finite; a program needn't handle non-finite values.
Results may differ from a plain program's by a relative error of at most 0.0031.
Values may be sent and summed in bfloat16 or wider, within the bound.
A program may use at most 64 MiB of HBM per device.

v0:
```python
import functools
import math

import jax
import jax.numpy as jnp
from jax import lax
from jax.experimental import pallas as pl
from jax.experimental.pallas import tpu as pltpu
from jax.sharding import PartitionSpec as P

QUERY_HEADS = 32
KEY_VALUE_HEADS = 4
HEAD_SIZE = 128
QUERIES_PER_KV = 8
CHUNK_HEADS = 2

MASK_FLOOR = -1e30
MESH = pl.DeviceIdType.MESH


def kernel(
    dp_count, ctx_count,
    qkv_ref, dest_ref, order_ref, lengths_ref,
    out_ref,
    q_buf, kv_buf, bias, own, from_below, from_above,
    local_sem, kv_send, kv_recv, out_send, out_recv,
):
    dp_index = lax.axis_index("dp")
    me = lax.axis_index("ctx")
    above = lax.rem(dp_index + 1, dp_count)
    below = lax.rem(dp_index + dp_count - 1, dp_count)
    rows = qkv_ref.shape[1]
    span = rows // 2
    docs = lengths_ref.shape[1]
    query_width = QUERY_HEADS * HEAD_SIZE
    chunk_cols = CHUNK_HEADS * HEAD_SIZE
    chunks = QUERY_HEADS // CHUNK_HEADS
    group_chunks = QUERIES_PER_KV // CHUNK_HEADS
    my_rows = pl.ds(pl.multiple_of(me * rows, rows), rows)

    local = []
    for g in range(KEY_VALUE_HEADS):
        for part in range(2):
            first = query_width + (part * KEY_VALUE_HEADS + g) * HEAD_SIZE
            copy = pltpu.make_async_copy(
                qkv_ref.at[0, :, pl.ds(first, HEAD_SIZE)],
                kv_buf.at[g, part, my_rows, :],
                local_sem.at[2 * g + part],
            )
            copy.start()
            local.append(copy)
    q_copy = pltpu.make_async_copy(
        qkv_ref.at[0, :, pl.ds(0, query_width)], q_buf, local_sem.at[2 * KEY_VALUE_HEADS]
    )
    q_copy.start()

    barrier = pltpu.get_barrier_semaphore()
    for k in range(1, ctx_count):
        pl.semaphore_signal(
            barrier, inc=1, device_id={"ctx": lax.rem(me + k, ctx_count)}, device_id_type=MESH
        )
    pl.semaphore_signal(barrier, inc=1, device_id={"dp": above}, device_id_type=MESH)
    pl.semaphore_signal(barrier, inc=1, device_id={"dp": below}, device_id_type=MESH)
    pl.semaphore_wait(barrier, ctx_count + 1)

    def kv_copy(g, k):
        peer = lax.rem(me + k, ctx_count)
        return pltpu.make_async_remote_copy(
            src_ref=kv_buf.at[g, :, my_rows, :],
            dst_ref=kv_buf.at[g, :, my_rows, :],
            send_sem=kv_send.at[g, k],
            recv_sem=kv_recv.at[g, k],
            device_id={"ctx": peer},
            device_id_type=MESH,
        )

    def kv_arrival(g, k):
        peer = lax.rem(me + ctx_count - k, ctx_count)
        its_rows = pl.ds(pl.multiple_of(peer * rows, rows), rows)
        landed = kv_buf.at[g, :, its_rows, :]
        return pltpu.make_async_remote_copy(
            src_ref=landed, dst_ref=landed, send_sem=kv_send.at[g, k], recv_sem=kv_recv.at[g, k],
            device_id={"ctx": peer}, device_id_type=MESH,
        )

    for g in range(KEY_VALUE_HEADS):
        local[2 * g].wait()
        local[2 * g + 1].wait()
        for k in range(1, ctx_count):
            kv_copy(g, k).start()

    ends = []
    total_length = 0
    for d in range(docs):
        total_length = total_length + lengths_ref[dp_index, d]
        ends.append(total_length)

    def identity_of(place, first_slot):
        early = place < span
        position = jnp.where(
            early, order_ref[first_slot] * span, order_ref[first_slot + 1] * span - span
        ) + place
        counted = jnp.where(early, dest_ref[0, first_slot] * docs, dest_ref[0, first_slot + 1] * docs)
        for end in ends:
            counted = counted + (position >= end).astype(jnp.int32)
        return position, counted

    query_place = lax.broadcasted_iota(jnp.int32, (rows, rows), 0)
    key_place = lax.broadcasted_iota(jnp.int32, (rows, rows), 1)
    query_position, query_document = identity_of(query_place, 2 * me)
    for b in range(ctx_count):
        key_position, key_document = identity_of(key_place, 2 * b)
        visible = (key_document == query_document) & (key_position <= query_position)
        bias[:, b * rows:(b + 1) * rows] = jnp.where(visible, 0.0, MASK_FLOOR)

    def out_copy(chunk, up):
        return pltpu.make_async_remote_copy(
            src_ref=own.at[chunk],
            dst_ref=(from_below if up else from_above).at[chunk],
            send_sem=out_send.at[up, chunk],
            recv_sem=out_recv.at[up, chunk],
            device_id={"dp": above if up else below},
            device_id_type=MESH,
        )

    def send(chunk):
        out_copy(chunk, 1).start()
        out_copy(chunk, 0).start()

    exponent_scale = math.log2(math.e) / math.sqrt(HEAD_SIZE)
    q_copy.wait()
    for g in range(KEY_VALUE_HEADS):
        for k in range(1, ctx_count):
            kv_arrival(g, k).wait_recv()

        def one_chunk(i, carry):
            chunk = g * group_chunks + i
            for j in range(CHUNK_HEADS):
                first = pl.multiple_of(chunk * chunk_cols + j * HEAD_SIZE, HEAD_SIZE)
                query = q_buf[:, pl.ds(first, HEAD_SIZE)]
                scores = lax.dot_general(
                    query, kv_buf[g, 0], (((1,), (1,)), ((), ())),
                    preferred_element_type=jnp.float32,
                ) + bias[...]
                row_max = jnp.max(scores, axis=1, keepdims=True)
                weights = jnp.exp2((scores - row_max) * exponent_scale)
                total = jnp.sum(weights, axis=1, keepdims=True)
                mixed = jnp.dot(
                    weights.astype(jnp.bfloat16), kv_buf[g, 1],
                    preferred_element_type=jnp.float32,
                )
                own[chunk, :, j * HEAD_SIZE:(j + 1) * HEAD_SIZE] = (mixed / total).astype(jnp.bfloat16)
                if j == 0:
                    if g == 0:
                        @pl.when(i > 0)
                        def _():
                            send(chunk - 1)
                    else:
                        send(chunk - 1)
            return carry

        lax.fori_loop(0, group_chunks, one_chunk, 0)
    send(chunks - 1)

    below_masks, above_masks = [], []
    for half in range(2):
        source = jnp.full((span, chunk_cols), dest_ref[0, 2 * me + half], jnp.int32)
        below_masks.append(source == below)
        above_masks.append(source == above)

    def settle(chunk, carry):
        out_copy(chunk, 1).wait_recv()
        out_copy(chunk, 0).wait_recv()
        first = pl.multiple_of(chunk * chunk_cols, chunk_cols)
        for half in range(2):
            part = pl.ds(half * span, span)
            kept = own[chunk, part, :].astype(jnp.float32)
            lower = from_below[chunk, part, :].astype(jnp.float32)
            upper = from_above[chunk, part, :].astype(jnp.float32)
            chosen = jnp.where(
                below_masks[half], lower, jnp.where(above_masks[half], upper, kept)
            )
            out_ref[0, part, pl.ds(first, chunk_cols)] = chosen.astype(jnp.bfloat16)
        return carry

    lax.fori_loop(0, chunks, settle, 0)

    for g in range(KEY_VALUE_HEADS):
        for k in range(1, ctx_count):
            kv_copy(g, k).wait_send()

    def drain(chunk, carry):
        out_copy(chunk, 1).wait_send()
        out_copy(chunk, 0).wait_send()
        return carry

    lax.fori_loop(0, chunks, drain, 0)


def on_device(dp_count, ctx_count, qkv, dest, order, lengths):
    rows = qkv.shape[1]
    query_width = QUERY_HEADS * HEAD_SIZE
    chunks = QUERY_HEADS // CHUNK_HEADS
    chunk_shape = (chunks, rows, CHUNK_HEADS * HEAD_SIZE)
    keys = ctx_count * rows
    return pl.pallas_call(
        functools.partial(kernel, dp_count, ctx_count),
        out_shape=jax.ShapeDtypeStruct((1, rows, query_width), jnp.bfloat16),
        in_specs=[
            pl.BlockSpec(memory_space=pl.ANY),
            pl.BlockSpec(memory_space=pltpu.SMEM),
            pl.BlockSpec(memory_space=pltpu.SMEM),
            pl.BlockSpec(memory_space=pltpu.SMEM),
        ],
        out_specs=pl.BlockSpec(memory_space=pltpu.VMEM),
        scratch_shapes=[
            pltpu.VMEM((rows, query_width), jnp.bfloat16),
            pltpu.VMEM((KEY_VALUE_HEADS, 2, keys, HEAD_SIZE), jnp.bfloat16),
            pltpu.VMEM((rows, keys), jnp.float32),
            pltpu.VMEM(chunk_shape, jnp.bfloat16),
            pltpu.VMEM(chunk_shape, jnp.bfloat16),
            pltpu.VMEM(chunk_shape, jnp.bfloat16),
            pltpu.SemaphoreType.DMA((2 * KEY_VALUE_HEADS + 1,)),
            pltpu.SemaphoreType.DMA((KEY_VALUE_HEADS, ctx_count)),
            pltpu.SemaphoreType.DMA((KEY_VALUE_HEADS, ctx_count)),
            pltpu.SemaphoreType.DMA((2, chunks)),
            pltpu.SemaphoreType.DMA((2, chunks)),
        ],
        compiler_params=pltpu.CompilerParams(collective_id=0, has_side_effects=True),
    )(qkv, dest, order, lengths)


def solution(mesh):
    return jax.shard_map(
        functools.partial(on_device, mesh.shape["dp"], mesh.shape["ctx"]),
        mesh=mesh,
        in_specs=(P("dp", "ctx", None), P("dp", None), P(), P()),
        out_specs=P("dp", "ctx", None),
        check_vma=False,
    )
```

profile of v0, /device:TPU:1, one launch (start us, length us, event | category | flops | bytes accessed | tf_op | source)
XLA Modules:
  0.0 39.5 jit_solution(8323963472783546686)
XLA Ops:
  0.0 37.2 %shard_map.46 = bf16[1,128,4096]{2,1,0:T(8,128)(2,1)} custom-call(bf16[1,128,5120]{2,1,0:T(8,128)(2,1)} %qkv_ref.1, s32[1,8]{1,0:T(1,128)} %dest_ref.1, s32[8]{0:T(128)} %order_ref.1, s32[8,8]{1,0:T(8,128)} %lengths_ref.1), custom_call_target="tpu_custom_call" | custom-call | tf_op jit(solution)/shard_map/pallas_call | solution.py:206
  37.2 2.3 %copy.6 = bf16[1,128,4096]{2,1,0:T(8,128)(2,1)} copy(bf16[1,128,4096]{2,1,0:T(8,128)(2,1)} %shard_map.46) | data formatting | bytes 2097152
where the time goes:
time: 40 us; the launch traced here: 39.5 us
  Pallas kernels  37.2 us (93%)
  local copies, waits for them, and re-layouts  2.29 us (6%)
    pallas_call x1, Pallas kernels, on_device(): pl.pallas_call(functools.partial(kernel, dp_count, ctx_count), out_shape=...  37.2 us
    unnamed x1, local copies, waits for them, and re-layouts  2.29 us

commit v1 on v0

--- a/solution.py
+++ b/solution.py
@@ -13,6 +13,7 @@
 HEAD_SIZE = 128
 QUERIES_PER_KV = 8
 CHUNK_HEADS = 2
+PLACE_PARTS = 4
 
 MASK_FLOOR = -1e30
 MESH = pl.DeviceIdType.MESH
@@ -20,10 +21,10 @@
 
 def kernel(
     dp_count, ctx_count,
-    qkv_ref, dest_ref, order_ref, lengths_ref,
+    qkv_ref, dest_hbm, order_hbm, lengths_hbm,
     out_ref,
-    q_buf, kv_buf, bias, own, from_below, from_above,
-    local_sem, kv_send, kv_recv, out_send, out_recv,
+    dest_ref, order_ref, lengths_ref, q_buf, kv_buf, bias, own, from_below, from_above,
+    local_sem, scalar_sem, kv_send, kv_recv, out_send, out_recv,
 ):
     dp_index = lax.axis_index("dp")
     me = lax.axis_index("ctx")
@@ -38,6 +39,19 @@
     group_chunks = QUERIES_PER_KV // CHUNK_HEADS
     my_rows = pl.ds(pl.multiple_of(me * rows, rows), rows)
 
+    barrier = pltpu.get_barrier_semaphore()
+    for k in range(1, ctx_count):
+        pl.semaphore_signal(
+            barrier, inc=1, device_id={"ctx": lax.rem(me + k, ctx_count)}, device_id_type=MESH
+        )
+    pl.semaphore_signal(barrier, inc=1, device_id={"dp": above}, device_id_type=MESH)
+    pl.semaphore_signal(barrier, inc=1, device_id={"dp": below}, device_id_type=MESH)
+    scalars = [
+        pltpu.make_async_copy(source, target, scalar_sem.at[i])
+        for i, (source, target) in enumerate(
+            ((dest_hbm, dest_ref), (order_hbm, order_ref), (lengths_hbm, lengths_ref))
+        )
+    ]
     local = []
     for g in range(KEY_VALUE_HEADS):
         for part in range(2):
@@ -53,14 +67,9 @@
         qkv_ref.at[0, :, pl.ds(0, query_width)], q_buf, local_sem.at[2 * KEY_VALUE_HEADS]
     )
     q_copy.start()
-
-    barrier = pltpu.get_barrier_semaphore()
-    for k in range(1, ctx_count):
-        pl.semaphore_signal(
-            barrier, inc=1, device_id={"ctx": lax.rem(me + k, ctx_count)}, device_id_type=MESH
-        )
-    pl.semaphore_signal(barrier, inc=1, device_id={"dp": above}, device_id_type=MESH)
-    pl.semaphore_signal(barrier, inc=1, device_id={"dp": below}, device_id_type=MESH)
+    for copy in scalars:
+        copy.start()
+
     pl.semaphore_wait(barrier, ctx_count + 1)
 
     def kv_copy(g, k):
@@ -88,6 +97,9 @@
         local[2 * g + 1].wait()
         for k in range(1, ctx_count):
             kv_copy(g, k).start()
+
+    for copy in scalars:
+        copy.wait()
 
     ends = []
     total_length = 0
@@ -197,23 +209,41 @@
     lax.fori_loop(0, chunks, drain, 0)
 
 
+def place_kernel(settled_ref, out_ref, sems):
+    rows = settled_ref.shape[1] // PLACE_PARTS
+    copies = [
+        pltpu.make_async_copy(
+            settled_ref.at[0, pl.ds(i * rows, rows), :],
+            out_ref.at[0, pl.ds(i * rows, rows), :],
+            sems.at[i],
+        )
+        for i in range(PLACE_PARTS)
+    ]
+    for copy in copies:
+        copy.start()
+    for copy in copies:
+        copy.wait()
+
+
 def on_device(dp_count, ctx_count, qkv, dest, order, lengths):
     rows = qkv.shape[1]
     query_width = QUERY_HEADS * HEAD_SIZE
     chunks = QUERY_HEADS // CHUNK_HEADS
     chunk_shape = (chunks, rows, CHUNK_HEADS * HEAD_SIZE)
     keys = ctx_count * rows
-    return pl.pallas_call(
+    qkv, dest, order, lengths = (
+        pltpu.with_memory_space_constraint(array, pltpu.HBM)
+        for array in (qkv, dest, order, lengths)
+    )
+    settled = pl.pallas_call(
         functools.partial(kernel, dp_count, ctx_count),
-        out_shape=jax.ShapeDtypeStruct((1, rows, query_width), jnp.bfloat16),
-        in_specs=[
-            pl.BlockSpec(memory_space=pl.ANY),
-            pl.BlockSpec(memory_space=pltpu.SMEM),
-            pl.BlockSpec(memory_space=pltpu.SMEM),
-            pl.BlockSpec(memory_space=pltpu.SMEM),
-        ],
+        out_shape=pltpu.VMEM((1, rows, query_width), jnp.bfloat16),
+        in_specs=[pl.BlockSpec(memory_space=pltpu.HBM)] * 4,
         out_specs=pl.BlockSpec(memory_space=pltpu.VMEM),
         scratch_shapes=[
+            pltpu.SMEM(dest.shape, jnp.int32),
+            pltpu.SMEM(order.shape, jnp.int32),
+            pltpu.SMEM(lengths.shape, jnp.int32),
             pltpu.VMEM((rows, query_width), jnp.bfloat16),
             pltpu.VMEM((KEY_VALUE_HEADS, 2, keys, HEAD_SIZE), jnp.bfloat16),
             pltpu.VMEM((rows, keys), jnp.float32),
@@ -221,13 +251,23 @@
             pltpu.VMEM(chunk_shape, jnp.bfloat16),
             pltpu.VMEM(chunk_shape, jnp.bfloat16),
             pltpu.SemaphoreType.DMA((2 * KEY_VALUE_HEADS + 1,)),
+            pltpu.SemaphoreType.DMA((3,)),
             pltpu.SemaphoreType.DMA((KEY_VALUE_HEADS, ctx_count)),
             pltpu.SemaphoreType.DMA((KEY_VALUE_HEADS, ctx_count)),
             pltpu.SemaphoreType.DMA((2, chunks)),
             pltpu.SemaphoreType.DMA((2, chunks)),
         ],
-        compiler_params=pltpu.CompilerParams(collective_id=0, has_side_effects=True),
+        compiler_params=pltpu.CompilerParams(collective_id=0, has_side_effects=True,
+            vmem_limit_bytes=40 << 20),
     )(qkv, dest, order, lengths)
+    return pl.pallas_call(
+        place_kernel,
+        out_shape=jax.ShapeDtypeStruct((1, rows, query_width), jnp.bfloat16),
+        in_specs=[pl.BlockSpec(memory_space=pltpu.VMEM)],
+        out_specs=pl.BlockSpec(memory_space=pltpu.HBM),
+        scratch_shapes=[pltpu.SemaphoreType.DMA((PLACE_PARTS,))],
+        compiler_params=pltpu.CompilerParams(vmem_limit_bytes=8 << 20),
+    )(settled)
 
 
 def solution(mesh):

time: 40 us -> 36.9 us (0.922)
  local copies, waits for them, and re-layouts: 2.29 us -> 0 us
  Pallas kernels: 37.2 us -> 36.4 us
    unnamed x1 -> x0, local copies, waits for them, and re-layouts: 2.29 us -> none
    pallas_call x1, Pallas kernels: 37.2 us -> 35.4 us  [on_device(): pl.pallas_call(functools.partial(kernel, dp_count, ctx_count), out_shape=...]
    pallas_call x0 -> x1, Pallas kernels: none -> 1 us  [on_device(): pl.pallas_call(place_kernel, out_shape=jax.ShapeDtypeStruct((1, rows, que...]
where the time goes in v1:
time: 36.9 us; the launch traced here: 36.4 us
  Pallas kernels  36.4 us (99%)
    pallas_call x1, Pallas kernels, on_device(): pl.pallas_call(functools.partial(kernel, dp_count, ctx_count), out_shape=...  35.4 us
    pallas_call x1, Pallas kernels, on_device(): pl.pallas_call(place_kernel, out_shape=jax.ShapeDtypeStruct((1, rows, que...  1 us

profile of v1, /device:TPU:1, one launch (start us, length us, event | category | flops | bytes accessed | tf_op | source)
XLA Modules:
  0.0 36.4 jit_solution(1527403963894191006)
XLA Ops:
  0.0 35.4 %shard_map.46.settled_ref = bf16[1,128,4096]{2,1,0:T(8,128)(2,1)S(1)} custom-call(bf16[1,128,5120]{2,1,0:T(8,128)(2,1)} %qkv_ref.1, s32[1,8]{1,0:T(1,128)} %dest_hbm.1, s32[8]{0:T(128)} %order_hbm.1, s32[8,8]{1,0:T(8,128)} %lengths_hbm.1), custom_call_target="tpu_custom_call" | custom-call | tf_op jit(solution)/shard_map/pallas_call | solution.py:238
  35.4 1.0 %shard_map.47 = bf16[1,128,4096]{2,1,0:T(8,128)(2,1)} custom-call(bf16[1,128,4096]{2,1,0:T(8,128)(2,1)S(1)} %shard_map.46.settled_ref), custom_call_target="tpu_custom_call" | custom-call | tf_op jit(solution)/shard_map/pallas_call | solution.py:263

commit v2 on v1

--- a/solution.py
+++ b/solution.py
@@ -23,8 +23,9 @@
     dp_count, ctx_count,
     qkv_ref, dest_hbm, order_hbm, lengths_hbm,
     out_ref,
-    dest_ref, order_ref, lengths_ref, q_buf, kv_buf, bias, own, from_below, from_above,
-    local_sem, scalar_sem, kv_send, kv_recv, out_send, out_recv,
+    dest_ref, order_ref, lengths_ref, q_buf, kv_buf, bias, settled_bias, own, from_below, from_above,
+    moved_q, moved_kv, own_kv,
+    local_sem, scalar_sem, kv_send, kv_recv, out_send, out_recv, moved_send, moved_recv,
 ):
     dp_index = lax.axis_index("dp")
     me = lax.axis_index("ctx")
@@ -35,8 +36,10 @@
     docs = lengths_ref.shape[1]
     query_width = QUERY_HEADS * HEAD_SIZE
     chunk_cols = CHUNK_HEADS * HEAD_SIZE
-    chunks = QUERY_HEADS // CHUNK_HEADS
+    moved = KEY_VALUE_HEADS - 1
     group_chunks = QUERIES_PER_KV // CHUNK_HEADS
+    chunks = moved * group_chunks
+    moved_cols = pl.ds(moved * QUERIES_PER_KV * HEAD_SIZE, QUERIES_PER_KV * HEAD_SIZE)
     my_rows = pl.ds(pl.multiple_of(me * rows, rows), rows)
 
     barrier = pltpu.get_barrier_semaphore()
@@ -53,20 +56,21 @@
         )
     ]
     local = []
-    for g in range(KEY_VALUE_HEADS):
+    for g in (moved, *range(moved)):
         for part in range(2):
             first = query_width + (part * KEY_VALUE_HEADS + g) * HEAD_SIZE
             copy = pltpu.make_async_copy(
                 qkv_ref.at[0, :, pl.ds(first, HEAD_SIZE)],
-                kv_buf.at[g, part, my_rows, :],
+                own_kv.at[part] if g == moved else kv_buf.at[g, part, my_rows, :],
                 local_sem.at[2 * g + part],
             )
             copy.start()
             local.append(copy)
-    q_copy = pltpu.make_async_copy(
-        qkv_ref.at[0, :, pl.ds(0, query_width)], q_buf, local_sem.at[2 * KEY_VALUE_HEADS]
-    )
-    q_copy.start()
+        if g == moved:
+            q_copy = pltpu.make_async_copy(
+                qkv_ref.at[0, :, pl.ds(0, query_width)], q_buf, local_sem.at[2 * KEY_VALUE_HEADS]
+            )
+            q_copy.start()
     for copy in scalars:
         copy.start()
 
@@ -92,38 +96,80 @@
             device_id={"ctx": peer}, device_id_type=MESH,
         )
 
-    for g in range(KEY_VALUE_HEADS):
-        local[2 * g].wait()
-        local[2 * g + 1].wait()
+    def moved_copy(kind, up):
+        return pltpu.make_async_remote_copy(
+            src_ref=q_buf.at[:, moved_cols] if kind else own_kv,
+            dst_ref=(moved_q if kind else moved_kv).at[up],
+            send_sem=moved_send.at[up, kind],
+            recv_sem=moved_recv.at[up, kind],
+            device_id={"dp": above if up else below},
+            device_id_type=MESH,
+        )
+
+    local[0].wait()
+    local[1].wait()
+    moved_copy(0, 1).start()
+    moved_copy(0, 0).start()
+    for g in range(moved):
+        local[2 * g + 2].wait()
+        local[2 * g + 3].wait()
         for k in range(1, ctx_count):
             kv_copy(g, k).start()
+        if g == 0:
+            q_copy.wait()
+            moved_copy(1, 1).start()
+            moved_copy(1, 0).start()
 
     for copy in scalars:
         copy.wait()
 
-    ends = []
-    total_length = 0
-    for d in range(docs):
-        total_length = total_length + lengths_ref[dp_index, d]
-        ends.append(total_length)
-
-    def identity_of(place, first_slot):
+    def ends_of(sequence):
+        ends = []
+        total_length = 0
+        for d in range(docs):
+            total_length = total_length + lengths_ref[sequence, d]
+            ends.append(total_length)
+        return ends
+
+    own_ends = ends_of(dp_index)
+
+    def identity_of(place, first_slot, settled):
         early = place < span
         position = jnp.where(
             early, order_ref[first_slot] * span, order_ref[first_slot + 1] * span - span
         ) + place
-        counted = jnp.where(early, dest_ref[0, first_slot] * docs, dest_ref[0, first_slot + 1] * docs)
+        partners = dest_ref[0, first_slot], dest_ref[0, first_slot + 1]
+        counted = jnp.where(early, partners[0] * docs, partners[1] * docs)
+        if settled:
+            ends = [jnp.where(early, *pair) for pair in zip(ends_of(partners[0]), ends_of(partners[1]))]
+        else:
+            ends = own_ends
         for end in ends:
             counted = counted + (position >= end).astype(jnp.int32)
         return position, counted
 
     query_place = lax.broadcasted_iota(jnp.int32, (rows, rows), 0)
-    key_place = lax.broadcasted_iota(jnp.int32, (rows, rows), 1)
-    query_position, query_document = identity_of(query_place, 2 * me)
-    for b in range(ctx_count):
-        key_position, key_document = identity_of(key_place, 2 * b)
-        visible = (key_document == query_document) & (key_position <= query_position)
-        bias[:, b * rows:(b + 1) * rows] = jnp.where(visible, 0.0, MASK_FLOOR)
+    key_place = lax.broadcasted_iota(jnp.int32, (1, rows), 1)
+    for settled, target in ((False, bias), (True, settled_bias)):
+        query_position, query_document = identity_of(query_place, 2 * me, settled)
+        for b in range(ctx_count):
+            key_position, key_document = identity_of(key_place, 2 * b, settled)
+            visible = (key_document == query_document) & (key_position <= query_position)
+            target[:, b * rows:(b + 1) * rows] = jnp.where(visible, 0.0, MASK_FLOOR)
+
+    row_source = jnp.where(
+        lax.broadcasted_iota(jnp.int32, (rows, HEAD_SIZE), 0) < span,
+        dest_ref[0, 2 * me], dest_ref[0, 2 * me + 1],
+    )
+    is_below = row_source == below
+    is_above = row_source == above
+
+    def settle_rows(kept, lower, upper):
+        chosen = jnp.where(
+            is_below, lower.astype(jnp.float32),
+            jnp.where(is_above, upper.astype(jnp.float32), kept.astype(jnp.float32)),
+        )
+        return chosen.astype(jnp.bfloat16)
 
     def out_copy(chunk, up):
         return pltpu.make_async_remote_copy(
@@ -140,8 +186,20 @@
         out_copy(chunk, 0).start()
 
     exponent_scale = math.log2(math.e) / math.sqrt(HEAD_SIZE)
-    q_copy.wait()
-    for g in range(KEY_VALUE_HEADS):
+
+    def attend(query, g, mask):
+        scores = lax.dot_general(
+            query, kv_buf[g, 0], (((1,), (1,)), ((), ())), preferred_element_type=jnp.float32
+        ) + mask[...]
+        row_max = jnp.max(scores, axis=1, keepdims=True)
+        weights = jnp.exp2((scores - row_max) * exponent_scale)
+        total = jnp.sum(weights, axis=1, keepdims=True)
+        mixed = jnp.dot(
+            weights.astype(jnp.bfloat16), kv_buf[g, 1], preferred_element_type=jnp.float32
+        )
+        return (mixed / total).astype(jnp.bfloat16)
+
+    for g in range(moved):
         for k in range(1, ctx_count):
             kv_arrival(g, k).wait_recv()
 
@@ -149,19 +207,9 @@
             chunk = g * group_chunks + i
             for j in range(CHUNK_HEADS):
                 first = pl.multiple_of(chunk * chunk_cols + j * HEAD_SIZE, HEAD_SIZE)
-                query = q_buf[:, pl.ds(first, HEAD_SIZE)]
-                scores = lax.dot_general(
-                    query, kv_buf[g, 0], (((1,), (1,)), ((), ())),
-                    preferred_element_type=jnp.float32,
-                ) + bias[...]
-                row_max = jnp.max(scores, axis=1, keepdims=True)
-                weights = jnp.exp2((scores - row_max) * exponent_scale)
-                total = jnp.sum(weights, axis=1, keepdims=True)
-                mixed = jnp.dot(
-                    weights.astype(jnp.bfloat16), kv_buf[g, 1],
-                    preferred_element_type=jnp.float32,
+                own[chunk, :, j * HEAD_SIZE:(j + 1) * HEAD_SIZE] = attend(
+                    q_buf[:, pl.ds(first, HEAD_SIZE)], g, bias
                 )
-                own[chunk, :, j * HEAD_SIZE:(j + 1) * HEAD_SIZE] = (mixed / total).astype(jnp.bfloat16)
                 if j == 0:
                     if g == 0:
                         @pl.when(i > 0)
@@ -171,32 +219,53 @@
                         send(chunk - 1)
             return carry
 
+        if g == moved - 1:
+            for k in range(1, ctx_count):
+                kv_copy(moved, k).start()
         lax.fori_loop(0, group_chunks, one_chunk, 0)
+        if g == max(moved - 2, 0):
+            moved_copy(0, 1).wait_recv()
+            moved_copy(0, 0).wait_recv()
+            for part in range(2):
+                kv_buf[moved, part, my_rows, :] = settle_rows(
+                    own_kv[part], moved_kv[1, part], moved_kv[0, part]
+                )
     send(chunks - 1)
 
-    below_masks, above_masks = [], []
-    for half in range(2):
-        source = jnp.full((span, chunk_cols), dest_ref[0, 2 * me + half], jnp.int32)
-        below_masks.append(source == below)
-        above_masks.append(source == above)
+    moved_copy(1, 1).wait_recv()
+    moved_copy(1, 0).wait_recv()
+    for k in range(1, ctx_count):
+        kv_arrival(moved, k).wait_recv()
+
+    def one_moved(i, carry):
+        for j in range(CHUNK_HEADS):
+            inner = pl.ds(pl.multiple_of(i * chunk_cols + j * HEAD_SIZE, HEAD_SIZE), HEAD_SIZE)
+            outer = pl.ds(
+                pl.multiple_of(chunks * chunk_cols + i * chunk_cols + j * HEAD_SIZE, HEAD_SIZE),
+                HEAD_SIZE,
+            )
+            query = settle_rows(q_buf[:, outer], moved_q[1, :, inner], moved_q[0, :, inner])
+            out_ref[0, :, outer] = attend(query, moved, settled_bias)
+        return carry
+
+    lax.fori_loop(0, group_chunks, one_moved, 0)
 
     def settle(chunk, carry):
         out_copy(chunk, 1).wait_recv()
         out_copy(chunk, 0).wait_recv()
-        first = pl.multiple_of(chunk * chunk_cols, chunk_cols)
-        for half in range(2):
-            part = pl.ds(half * span, span)
-            kept = own[chunk, part, :].astype(jnp.float32)
-            lower = from_below[chunk, part, :].astype(jnp.float32)
-            upper = from_above[chunk, part, :].astype(jnp.float32)
-            chosen = jnp.where(
-                below_masks[half], lower, jnp.where(above_masks[half], upper, kept)
+        for j in range(CHUNK_HEADS):
+            first = pl.multiple_of(chunk * chunk_cols + j * HEAD_SIZE, HEAD_SIZE)
+            part = pl.ds(j * HEAD_SIZE, HEAD_SIZE)
+            out_ref[0, :, pl.ds(first, HEAD_SIZE)] = settle_rows(
+                own[chunk, :, part], from_below[chunk, :, part], from_above[chunk, :, part]
             )
-            out_ref[0, part, pl.ds(first, chunk_cols)] = chosen.astype(jnp.bfloat16)
         return carry
 
     lax.fori_loop(0, chunks, settle, 0)
 
+    for kind in range(2):
+        for up in range(2):
+            moved_copy(kind, up).wait_send()
     for g in range(KEY_VALUE_HEADS):
         for k in range(1, ctx_count):
             kv_copy(g, k).wait_send()
@@ -228,7 +297,8 @@
 def on_device(dp_count, ctx_count, qkv, dest, order, lengths):
     rows = qkv.shape[1]
     query_width = QUERY_HEADS * HEAD_SIZE
-    chunks = QUERY_HEADS // CHUNK_HEADS
+    group_width = QUERIES_PER_KV * HEAD_SIZE
+    chunks = (QUERY_HEADS - QUERIES_PER_KV) // CHUNK_HEADS
     chunk_shape = (chunks, rows, CHUNK_HEADS * HEAD_SIZE)
     keys = ctx_count * rows
     qkv, dest, order, lengths = (
@@ -247,15 +317,21 @@
             pltpu.VMEM((rows, query_width), jnp.bfloat16),
             pltpu.VMEM((KEY_VALUE_HEADS, 2, keys, HEAD_SIZE), jnp.bfloat16),
             pltpu.VMEM((rows, keys), jnp.float32),
+            pltpu.VMEM((rows, keys), jnp.float32),
             pltpu.VMEM(chunk_shape, jnp.bfloat16),
             pltpu.VMEM(chunk_shape, jnp.bfloat16),
             pltpu.VMEM(chunk_shape, jnp.bfloat16),
+            pltpu.VMEM((2, rows, group_width), jnp.bfloat16),
+            pltpu.VMEM((2, 2, rows, HEAD_SIZE), jnp.bfloat16),
+            pltpu.VMEM((2, rows, HEAD_SIZE), jnp.bfloat16),
             pltpu.SemaphoreType.DMA((2 * KEY_VALUE_HEADS + 1,)),
             pltpu.SemaphoreType.DMA((3,)),
             pltpu.SemaphoreType.DMA((KEY_VALUE_HEADS, ctx_count)),
             pltpu.SemaphoreType.DMA((KEY_VALUE_HEADS, ctx_count)),
             pltpu.SemaphoreType.DMA((2, chunks)),
             pltpu.SemaphoreType.DMA((2, chunks)),
+            pltpu.SemaphoreType.DMA((2, 2)),
+            pltpu.SemaphoreType.DMA((2, 2)),
         ],
         compiler_params=pltpu.CompilerParams(collective_id=0, has_side_effects=True,
             vmem_limit_bytes=40 << 20),

time: 36.9 us -> 32.8 us (0.89)
  Pallas kernels: 36.4 us -> 32.3 us
    pallas_call x1, Pallas kernels: 35.4 us -> 31.3 us  [on_device(): pl.pallas_call(functools.partial(kernel, dp_count, ctx_count), out_shape=...]
where the time goes in v2:
time: 32.8 us; the launch traced here: 32.3 us
  Pallas kernels  32.3 us (98%)
    pallas_call x1, Pallas kernels, on_device(): pl.pallas_call(functools.partial(kernel, dp_count, ctx_count), out_shape=...  31.3 us
    pallas_call x1, Pallas kernels, on_device(): pl.pallas_call(place_kernel, out_shape=jax.ShapeDtypeStruct((1, rows, que...  1 us

profile of v2, /device:TPU:1, one launch (start us, length us, event | category | flops | bytes accessed | tf_op | source)
XLA Modules:
  0.0 32.3 jit_solution(16701077057624703347)
XLA Ops:
  0.0 31.3 %shard_map.46.settled_ref = bf16[1,128,4096]{2,1,0:T(8,128)(2,1)S(1)} custom-call(bf16[1,128,5120]{2,1,0:T(8,128)(2,1)} %qkv_ref.1, s32[1,8]{1,0:T(1,128)} %dest_hbm.1, s32[8]{0:T(128)} %order_hbm.1, s32[8,8]{1,0:T(8,128)} %lengths_hbm.1), custom_call_target="tpu_custom_call" | custom-call | tf_op jit(solution)/shard_map/pallas_call | solution.py:308
  31.3 1.0 %shard_map.47 = bf16[1,128,4096]{2,1,0:T(8,128)(2,1)} custom-call(bf16[1,128,4096]{2,1,0:T(8,128)(2,1)S(1)} %shard_map.46.settled_ref), custom_call_target="tpu_custom_call" | custom-call | tf_op jit(solution)/shard_map/pallas_call | solution.py:339

commit v3 on v2

--- a/solution.py
+++ b/solution.py
@@ -12,7 +12,7 @@
 KEY_VALUE_HEADS = 4
 HEAD_SIZE = 128
 QUERIES_PER_KV = 8
-CHUNK_HEADS = 2
+CHUNK_HEADS = 4
 PLACE_PARTS = 4
 
 MASK_FLOOR = -1e30
@@ -43,12 +43,12 @@
     my_rows = pl.ds(pl.multiple_of(me * rows, rows), rows)
 
     barrier = pltpu.get_barrier_semaphore()
+    pl.semaphore_signal(barrier, inc=1, device_id={"dp": above}, device_id_type=MESH)
+    pl.semaphore_signal(barrier, inc=1, device_id={"dp": below}, device_id_type=MESH)
     for k in range(1, ctx_count):
         pl.semaphore_signal(
             barrier, inc=1, device_id={"ctx": lax.rem(me + k, ctx_count)}, device_id_type=MESH
         )
-    pl.semaphore_signal(barrier, inc=1, device_id={"dp": above}, device_id_type=MESH)
-    pl.semaphore_signal(barrier, inc=1, device_id={"dp": below}, device_id_type=MESH)
     scalars = [
         pltpu.make_async_copy(source, target, scalar_sem.at[i])
         for i, (source, target) in enumerate(

time: 32.8 us -> 32.4 us (0.988)
  no operation moved by 1% of the time
where the time goes in v3:
time: 32.4 us; the launch traced here: 32 us
  Pallas kernels  32 us (99%)
    pallas_call x1, Pallas kernels, on_device(): pl.pallas_call(functools.partial(kernel, dp_count, ctx_count), out_shape=...  31 us
    pallas_call x1, Pallas kernels, on_device(): pl.pallas_call(place_kernel, out_shape=jax.ShapeDtypeStruct((1, rows, que...  1 us

profile of v3, /device:TPU:1, one launch (start us, length us, event | category | flops | bytes accessed | tf_op | source)
XLA Modules:
  0.0 32.0 jit_solution(10736383344470878242)
XLA Ops:
  0.0 31.0 %shard_map.46.settled_ref = bf16[1,128,4096]{2,1,0:T(8,128)(2,1)S(1)} custom-call(bf16[1,128,5120]{2,1,0:T(8,128)(2,1)} %qkv_ref.1, s32[1,8]{1,0:T(1,128)} %dest_hbm.1, s32[8]{0:T(128)} %order_hbm.1, s32[8,8]{1,0:T(8,128)} %lengths_hbm.1), custom_call_target="tpu_custom_call" | custom-call | tf_op jit(solution)/shard_map/pallas_call | solution.py:308
  31.0 1.0 %shard_map.47 = bf16[1,128,4096]{2,1,0:T(8,128)(2,1)} custom-call(bf16[1,128,4096]{2,1,0:T(8,128)(2,1)S(1)} %shard_map.46.settled_ref), custom_call_target="tpu_custom_call" | custom-call | tf_op jit(solution)/shard_map/pallas_call | solution.py:339

commit v4 on v3

--- a/solution.py
+++ b/solution.py
@@ -25,7 +25,7 @@
     out_ref,
     dest_ref, order_ref, lengths_ref, q_buf, kv_buf, bias, settled_bias, own, from_below, from_above,
     moved_q, moved_kv, own_kv,
-    local_sem, scalar_sem, kv_send, kv_recv, out_send, out_recv, moved_send, moved_recv,
+    local_sem, scalar_sem, kv_send, kv_recv, out_send, out_recv, moved_send, moved_recv, corner_sem,
 ):
     dp_index = lax.axis_index("dp")
     me = lax.axis_index("ctx")
@@ -42,13 +42,22 @@
     moved_cols = pl.ds(moved * QUERIES_PER_KV * HEAD_SIZE, QUERIES_PER_KV * HEAD_SIZE)
     my_rows = pl.ds(pl.multiple_of(me * rows, rows), rows)
 
+    square = ctx_count == 4
+    corner = 3
+
+    def target_of(k):
+        if square:
+            return (me + 1 - 2 * lax.rem(me, 2), lax.rem(me + 2, 4), 3 - me)[k - 1]
+        return lax.rem(me + k, ctx_count)
+
+    def origin_of(k):
+        return target_of(k) if square else lax.rem(me + ctx_count - k, ctx_count)
+
     barrier = pltpu.get_barrier_semaphore()
     pl.semaphore_signal(barrier, inc=1, device_id={"dp": above}, device_id_type=MESH)
     pl.semaphore_signal(barrier, inc=1, device_id={"dp": below}, device_id_type=MESH)
-    for k in range(1, ctx_count):
-        pl.semaphore_signal(
-            barrier, inc=1, device_id={"ctx": lax.rem(me + k, ctx_count)}, device_id_type=MESH
-        )
+    for k in range(1, corner if square else ctx_count):
+        pl.semaphore_signal(barrier, inc=1, device_id={"ctx": target_of(k)}, device_id_type=MESH)
     scalars = [
         pltpu.make_async_copy(source, target, scalar_sem.at[i])
         for i, (source, target) in enumerate(
@@ -74,10 +83,12 @@
     for copy in scalars:
         copy.start()
 
-    pl.semaphore_wait(barrier, ctx_count + 1)
+    pl.semaphore_wait(barrier, 4 if square else ctx_count + 1)
+    if square:
+        pl.semaphore_signal(corner_sem, inc=1, device_id={"ctx": target_of(1)}, device_id_type=MESH)
 
     def kv_copy(g, k):
-        peer = lax.rem(me + k, ctx_count)
+        peer = target_of(k)
         return pltpu.make_async_remote_copy(
             src_ref=kv_buf.at[g, :, my_rows, :],
             dst_ref=kv_buf.at[g, :, my_rows, :],
@@ -88,7 +99,7 @@
         )
 
     def kv_arrival(g, k):
-        peer = lax.rem(me + ctx_count - k, ctx_count)
+        peer = origin_of(k)
         its_rows = pl.ds(pl.multiple_of(peer * rows, rows), rows)
         landed = kv_buf.at[g, :, its_rows, :]
         return pltpu.make_async_remote_copy(
@@ -114,11 +125,13 @@
         local[2 * g + 2].wait()
         local[2 * g + 3].wait()
         for k in range(1, ctx_count):
+            if g == 0 and k == ctx_count - 1:
+                q_copy.wait()
+                moved_copy(1, 1).start()
+                moved_copy(1, 0).start()
+                if square:
+                    pl.semaphore_wait(corner_sem, 1)
             kv_copy(g, k).start()
-        if g == 0:
-            q_copy.wait()
-            moved_copy(1, 1).start()
-            moved_copy(1, 0).start()
 
     for copy in scalars:
         copy.wait()
@@ -332,6 +345,7 @@
             pltpu.SemaphoreType.DMA((2, chunks)),
             pltpu.SemaphoreType.DMA((2, 2)),
             pltpu.SemaphoreType.DMA((2, 2)),
+            pltpu.SemaphoreType.REGULAR,
         ],
         compiler_params=pltpu.CompilerParams(collective_id=0, has_side_effects=True,
             vmem_limit_bytes=40 << 20),

time: 32.4 us -> 32.2 us (level)
  no operation moved by 1% of the time
where the time goes in v4:
time: 32.2 us; the launch traced here: 32 us
  Pallas kernels  32 us (99%)
    pallas_call x1, Pallas kernels, on_device(): pl.pallas_call(functools.partial(kernel, dp_count, ctx_count), out_shape=...  31 us
    pallas_call x1, Pallas kernels, on_device(): pl.pallas_call(place_kernel, out_shape=jax.ShapeDtypeStruct((1, rows, que...  1 us

profile of v4, /device:TPU:1, one launch (start us, length us, event | category | flops | bytes accessed | tf_op | source)
XLA Modules:
  0.0 32.0 jit_solution(724420133928795413)
XLA Ops:
  0.0 31.0 %shard_map.46.settled_ref = bf16[1,128,4096]{2,1,0:T(8,128)(2,1)S(1)} custom-call(bf16[1,128,5120]{2,1,0:T(8,128)(2,1)} %qkv_ref.1, s32[1,8]{1,0:T(1,128)} %dest_hbm.1, s32[8]{0:T(128)} %order_hbm.1, s32[8,8]{1,0:T(8,128)} %lengths_hbm.1), custom_call_target="tpu_custom_call" | custom-call | tf_op jit(solution)/shard_map/pallas_call | solution.py:321
  31.0 1.0 %shard_map.47 = bf16[1,128,4096]{2,1,0:T(8,128)(2,1)} custom-call(bf16[1,128,4096]{2,1,0:T(8,128)(2,1)S(1)} %shard_map.46.settled_ref), custom_call_target="tpu_custom_call" | custom-call | tf_op jit(solution)/shard_map/pallas_call | solution.py:353
